TPU v7x, 8 devices: a whole 2x2x1 slice. The times are simulated.
8 devices in a mesh: tp: 8 (over z, y, x, core).
Axes of the slice: x: 2, y: 2, z: 1, core: 2. Of those that a mesh axis runs over, the one named last changes fastest.
Arguments:
- x_in: bfloat16 [16, 256, 2560], P(None, 'tp')
- grad_y: bfloat16 [16, 256, 2560], P(None, 'tp')
- ln_gain: float32 [2560], replicated
- w_query: bfloat16 [2560, 32, 80], P(None, 'tp')
- w_key: bfloat16 [2560, 80], replicated
- w_value: bfloat16 [2560, 80], replicated
- w_out: bfloat16 [32, 80, 2560], P('tp')
- w_gate: bfloat16 [2560, 10240], P(None, 'tp')
- w_up: bfloat16 [2560, 10240], P(None, 'tp')
- w_down: bfloat16 [10240, 2560], P('tp')
Outputs:
- output 1: bfloat16 [16, 256, 2560], P(None, 'tp')
- output 2: bfloat16 [16, 256, 2560], P(None, 'tp')
- output 3: float32 [2560], replicated
- output 4: bfloat16 [2560, 32, 80], P(None, 'tp')
- output 5: bfloat16 [2560, 80], replicated
- output 6: bfloat16 [2560, 80], replicated
- output 7: bfloat16 [32, 80, 2560], P('tp')
- output 8: bfloat16 [2560, 10240], P(None, 'tp')
- output 9: bfloat16 [2560, 10240], P(None, 'tp')
- output 10: bfloat16 [10240, 2560], P('tp')
All inputs are finite; a program needn't handle non-finite values.
Results may differ from a plain program's by a relative error of at most 0.0155186.
Values are sent between devices in bfloat16 or wider.
A program may use at most 1 GiB of HBM per device.

v0:
```python
import jax
import jax.numpy as jnp
from jax import lax
from jax.sharding import PartitionSpec as P

LN_EPS = 1e-6
ROPE_BASE = 10000.0


def rope_tables(seq_len, head_dim):
    half_dim = head_dim // 2
    inv_freq = ROPE_BASE ** (-jnp.arange(half_dim, dtype=jnp.float32) * 2.0 / head_dim)
    angles = jnp.arange(seq_len, dtype=jnp.float32)[:, None] * inv_freq[None, :]
    return jnp.cos(angles), jnp.sin(angles)


def rotate_half(values, cos_tab, sin_tab):
    half_dim = values.shape[-1] // 2
    first_half = values[..., :half_dim]
    second_half = values[..., half_dim:]
    return jnp.concatenate([first_half * cos_tab - second_half * sin_tab, second_half * cos_tab + first_half * sin_tab], axis=-1)


def solution(mesh):
    group_size = mesh.shape["tp"]

    def layer_shard(x_loc, grad_y_loc, ln_gain, w_query, w_key, w_value, w_out, w_gate, w_up, w_down):
        head_dim = w_key.shape[1]
        seq_len = x_loc.shape[1] * group_size
        score_scale = head_dim ** -0.5
        residual = x_loc.astype(jnp.float32)
        centered = residual - jnp.mean(residual, axis=-1, keepdims=True)
        inv_std = lax.rsqrt(jnp.mean(centered * centered, axis=-1, keepdims=True) + LN_EPS)
        x_hat = centered * inv_std
        normed_loc = (ln_gain * x_hat).astype(jnp.bfloat16)
        normed = lax.all_gather(normed_loc, "tp", axis=1, tiled=True)

        cos_tab, sin_tab = rope_tables(seq_len, head_dim)
        cos_head = cos_tab[:, None, :]
        sin_head = sin_tab[:, None, :]
        q_raw = jnp.einsum("bld,dnk->blnk", normed, w_query, preferred_element_type=jnp.float32)
        k_raw = jnp.einsum("bld,dk->blk", normed, w_key, preferred_element_type=jnp.float32)
        values = jnp.einsum("bld,dk->blk", normed, w_value, preferred_element_type=jnp.float32).astype(jnp.bfloat16)
        q_rot = rotate_half(q_raw, cos_head, sin_head).astype(jnp.bfloat16)
        k_rot = rotate_half(k_raw, cos_tab, sin_tab).astype(jnp.bfloat16)
        scores = jnp.einsum("bqnk,bsk->bnqs", q_rot, k_rot, preferred_element_type=jnp.float32) * score_scale
        positions = jnp.arange(seq_len)
        causal = positions[:, None] >= positions[None, :]
        attn_probs = jax.nn.softmax(jnp.where(causal, scores, -1e30), axis=-1)
        probs_low = attn_probs.astype(jnp.bfloat16)
        attn_heads = jnp.einsum("bnqs,bsk->bqnk", probs_low, values, preferred_element_type=jnp.float32).astype(jnp.bfloat16)
        attn_part = jnp.einsum("crol,ole->cre", attn_heads, w_out, preferred_element_type=jnp.float32)
        gate_pre = jnp.einsum("bld,df->blf", normed, w_gate, preferred_element_type=jnp.float32)
        up_pre = jnp.einsum("bld,df->blf", normed, w_up, preferred_element_type=jnp.float32)
        gate_sig = jax.nn.sigmoid(gate_pre)
        gate_act = gate_pre * gate_sig
        hidden = (gate_act * up_pre).astype(jnp.bfloat16)
        mlp_part = jnp.einsum("blf,fd->bld", hidden, w_down, preferred_element_type=jnp.float32)
        branch_part = (attn_part + mlp_part).astype(jnp.bfloat16)
        branch_loc = lax.psum_scatter(branch_part, "tp", scatter_dimension=1, tiled=True)
        y_loc = (residual + branch_loc.astype(jnp.float32)).astype(jnp.bfloat16)

        grad_full = lax.all_gather(grad_y_loc, "tp", axis=1, tiled=True)
        grad_hidden = jnp.einsum("bld,fd->blf", grad_full, w_down, preferred_element_type=jnp.float32)
        grad_w_down = jnp.einsum("blf,bld->fd", hidden, grad_full, preferred_element_type=jnp.float32)
        grad_gate = (grad_hidden * up_pre * gate_sig * (1.0 + gate_pre * (1.0 - gate_sig))).astype(jnp.bfloat16)
        grad_up = (grad_hidden * gate_act).astype(jnp.bfloat16)
        grad_w_gate = jnp.einsum("bld,blf->df", normed, grad_gate, preferred_element_type=jnp.float32)
        grad_w_up = jnp.einsum("bld,blf->df", normed, grad_up, preferred_element_type=jnp.float32)

        grad_heads = jnp.einsum("bld,nkd->blnk", grad_full, w_out, preferred_element_type=jnp.float32).astype(jnp.bfloat16)
        grad_w_out = jnp.einsum("blnk,bld->nkd", attn_heads, grad_full, preferred_element_type=jnp.float32)
        grad_probs = jnp.einsum("bqnk,bsk->bnqs", grad_heads, values, preferred_element_type=jnp.float32)
        grad_values = jnp.einsum("bnqs,bqnk->bsk", probs_low, grad_heads, preferred_element_type=jnp.float32).astype(jnp.bfloat16)
        row_dot = jnp.sum(attn_probs * grad_probs, axis=-1, keepdims=True)
        grad_scores = (attn_probs * (grad_probs - row_dot) * score_scale).astype(jnp.bfloat16)
        grad_q_rot = jnp.einsum("bnqs,bsk->bqnk", grad_scores, k_rot, preferred_element_type=jnp.float32)
        grad_k_rot = jnp.einsum("bnqs,bqnk->bsk", grad_scores, q_rot, preferred_element_type=jnp.float32)
        grad_query = rotate_half(grad_q_rot, cos_head, -sin_head).astype(jnp.bfloat16)
        grad_key = rotate_half(grad_k_rot, cos_tab, -sin_tab).astype(jnp.bfloat16)
        grad_w_query = jnp.einsum("bld,blnk->dnk", normed, grad_query, preferred_element_type=jnp.float32)
        grad_w_key = lax.psum(jnp.einsum("bld,blk->dk", normed, grad_key, preferred_element_type=jnp.float32), "tp")
        grad_w_value = lax.psum(jnp.einsum("bld,blk->dk", normed, grad_values, preferred_element_type=jnp.float32), "tp")

        grad_normed = (
            jnp.einsum("blf,df->bld", grad_gate, w_gate, preferred_element_type=jnp.float32)
            + jnp.einsum("blf,df->bld", grad_up, w_up, preferred_element_type=jnp.float32)
            + jnp.einsum("blnk,dnk->bld", grad_query, w_query, preferred_element_type=jnp.float32)
            + jnp.einsum("blk,dk->bld", grad_key, w_key, preferred_element_type=jnp.float32)
            + jnp.einsum("blk,dk->bld", grad_values, w_value, preferred_element_type=jnp.float32)
        ).astype(jnp.bfloat16)
        grad_normed_loc = lax.psum_scatter(grad_normed, "tp", scatter_dimension=1, tiled=True).astype(jnp.float32)
        grad_gain = lax.psum(jnp.sum(grad_normed_loc * x_hat, axis=(0, 1)), "tp")
        grad_hat = grad_normed_loc * ln_gain
        grad_x = inv_std * (grad_hat - jnp.mean(grad_hat, axis=-1, keepdims=True) - x_hat * jnp.mean(grad_hat * x_hat, axis=-1, keepdims=True)) + grad_y_loc.astype(jnp.float32)
        return (
            y_loc,
            grad_x.astype(jnp.bfloat16),
            grad_gain,
            grad_w_query.astype(jnp.bfloat16),
            grad_w_key.astype(jnp.bfloat16),
            grad_w_value.astype(jnp.bfloat16),
            grad_w_out.astype(jnp.bfloat16),
            grad_w_gate.astype(jnp.bfloat16),
            grad_w_up.astype(jnp.bfloat16),
            grad_w_down.astype(jnp.bfloat16),
        )

    act_spec = P(None, "tp", None)
    weight_specs = (P(), P(None, "tp", None), P(), P(), P("tp", None, None), P(None, "tp"), P(None, "tp"), P("tp", None))
    return jax.shard_map(layer_shard, mesh=mesh, in_specs=(act_spec, act_spec) + weight_specs, out_specs=(act_spec, act_spec) + weight_specs, check_vma=False)
```

profile of v0, /device:TPU:0, one launch (start us, length us, event | category | flops | bytes accessed | tf_op | source)
XLA Modules:
  0.0 882.5 jit_solution(9366745291565710666)
XLA Ops:
  7.2 0.0 all-gather.3.cloned.1.call-start
  7.3 2.3 convert_reduce_fusion
  9.6 2.6 fusion.47
  12.2 0.6 copy-done.27
  12.8 3.0 fusion.42
  15.9 0.0 all-gather.5.cloned.1.call-start
  15.9 0.7 all-gather.5.cloned.1.call-update
  16.6 0.2 reduce-scatter.5.cloned.1.call-start
  16.9 0.2 fusion.100
  17.1 103.6 %all-gather.3.cloned.1.call-done = bf16[16,256,2560]{2,1,0:T(8,128)(2,1)} async-done(((bf16[16,32,2560]{2,1,0:T(8,128)(2,1)}), bf16[16,256,2560]{2,1,0:T(8,128)(2,1)}) %all-gather.3.cloned.1.call-update) | async-done | bytes 20971536 | tf_op jit(solution)/shard_map/all_gather | solution.py:36
  120.7 13.1 %fusion.93 = f32[16,256,80]{1,2,0:T(8,128)S(1)} fusion(bf16[16,256,2560]{2,1,0:T(8,128)(2,1)} %all-gather.3.cloned.1.call-done, bf16[2560,80]{0,1:T(8,128)(2,1)S(1)} %copy-done.15), kind=kOutput, calls=%fused_computation.111 | convolution fusion | flops 1677721600 | bytes 22691840 | tf_op jit(solution)/shard_map/bld,dk->blk/dot_general | solution.py:42
  133.8 0.2 subtract_convert_fusion.3
  134.1 8.7 fusion.8
  142.7 4.9 subtract_convert_fusion.1
  147.6 6.4 fusion.90
  154.0 70.4 %all-gather.5.cloned.1.call-done = bf16[16,256,2560]{2,1,0:T(8,128)(2,1)} async-done(((bf16[16,32,2560]{2,1,0:T(8,128)(2,1)}), bf16[16,256,2560]{2,1,0:T(8,128)(2,1)}) %all-gather.5.cloned.1.call-update) | async-done | bytes 20971536 | tf_op jit(solution)/shard_map/all_gather | solution.py:63
  224.4 11.8 %fusion.74 = bf16[16,256,4,80]{1,3,2,0:T(8,128)(2,1)S(1)} fusion(bf16[16,256,2560]{2,1,0:T(8,128)(2,1)} %all-gather.5.cloned.1.call-done, bf16[4,80,2560]{2,1,0:T(8,128)(2,1)} %param.16), kind=kOutput, calls=%fused_computation.91 | convolution fusion | flops 6712197120 | bytes 25231360 | tf_op jit(solution)/shard_map/bld,nkd->blnk/dot_general | solution.py:71
  236.3 8.2 fusion.115
  244.5 8.1 fusion.78
  252.6 17.8 %fusion.114 = (f32[16,4,256]{2,1,0:T(4,128)S(1)}, f32[16,4,256,256]{2,3,1,0:T(8,128)}) fusion(f32[16,256,256,4]{2,1,3,0:T(8,128)} %fusion.78, pred[256,256]{0,1:T(8,128)(4,1)S(1)} %iota_compare_fusion), kind=kOutput, calls=%fused_computation.139 | output fusion | flops 25166080 | bytes 33685504 | tf_op jit(solution)/shard_map/sub | solution.py:49
  270.5 10.1 %fusion.87 = bf16[16,256,80]{1,2,0:T(8,128)(2,1)} fusion(bf16[16,256,4,80]{1,3,2,0:T(8,128)(2,1)} %copy-done.4, f32[16,4,256,256]{2,3,1,0:T(8,128)} %get-tuple-element.33, f32[16,4,256]{2,1,0:T(4,128)S(1)} %get-tuple-element.32), kind=kOutput, calls=%fused_computation.100 | convolution fusion | flops 679804928 | bytes 20119552 | tf_op jit(solution)/shard_map/bnqs,bqnk->bsk/dot_general | solution.py:74
  280.6 23.4 %fusion.86 = f32[16,256,80]{1,2,0:T(8,128)} fusion(bf16[16,256,4,40]{1,3,2,0:T(8,128)(2,1)} %get-tuple-element.22, bf16[16,256,4,40]{1,3,2,0:T(8,128)(2,1)S(1)} %copy-done.8, f32[16,256,256,4]{2,1,3,0:T(8,128)} %fusion.115, f32[16,4,256,256]{2,3,1,0:T(8,128)} %get-tuple-element.33, f32[16,4,256]{2,1,0:T(4,128)S(1)} %get-tuple-element.32), kind=kOutput, calls=%fused_computation.99 | convolution fusion | flops 705708288 | bytes 37552128 | tf_op jit(solution)/shard_map/bnqs,bqnk->bsk/dot_general | solution.py:78
  304.0 24.9 %fusion.70 = f32[16,256,4,80]{1,3,2,0:T(8,128)} fusion(f32[16,256,256,4]{2,1,3,0:T(8,128)} %fusion.115, bf16[16,256,40]{1,2,0:T(8,128)(2,1)} %copy-done.24, bf16[16,256,40]{1,2,0:T(8,128)(2,1)S(1)} %get-tuple-element.27, f32[16,4,256,256]{2,3,1,0:T(8,128)} %get-tuple-element.33, f32[16,4,256]{2,1,0:T(4,128)S(1)} %get-tuple-element.32), kind=kOutput, calls=%fused_computation.89 | convolution fusion | flops 701776128 | bytes 39518208 | tf_op jit(solution)/shard_map/bnqs,bsk->bqnk/dot_general | solution.py:77
  329.0 5.0 subtract_convert_fusion
  333.9 1.0 subtract_convert_fusion.2
  335.0 34.6 %fusion.27 = f32[16,256,1280]{2,1,0:T(8,128)} fusion(bf16[16,256,2560]{2,1,0:T(8,128)(2,1)} %all-gather.3.cloned.1.call-done, bf16[2560,1280]{1,0:T(8,128)(2,1)} %param.18), kind=kOutput, calls=%fused_computation.44 | convolution fusion | flops 26843545600 | bytes 48496640 | tf_op jit(solution)/shard_map/bld,df->blf/dot_general | solution.py:54
  369.6 31.6 %fusion.31 = f32[16,256,1280]{2,1,0:T(8,128)} fusion(bf16[16,256,2560]{2,1,0:T(8,128)(2,1)S(1)} %bitcast.185, bf16[2560,1280]{1,0:T(8,128)(2,1)} %param.17), kind=kOutput, calls=%fused_computation.48 | convolution fusion | flops 26843545600 | bytes 48496640 | tf_op jit(solution)/shard_map/bld,df->blf/dot_general | solution.py:53
  401.2 44.2 %multiply_convert_fusion = (bf16[16,256,1280]{2,1,0:T(8,128)(2,1)}, bf16[16,256,1280]{2,1,0:T(8,128)(2,1)}, bf16[16,256,1280]{2,1,0:T(8,128)(2,1)}) fusion(f32[16,256,1280]{2,1,0:T(8,128)} %fusion.31, f32[16,256,1280]{2,1,0:T(8,128)} %fusion.27, bf16[16,256,2560]{2,1,0:T(8,128)(2,1)} %all-gather.5.cloned.1.call-done, bf16[1280,2560]{1,0:T(8,128)(2,1)} %param.19), kind=kOutput, calls=%fused_computation.16 | convolution fusion | flops 26922188800 | bytes 100925440 | tf_op jit(solution)/shard_map/bld,fd->blf/dot_general | solution.py:64
  445.5 35.6 %fusion.29 = f32[16,256,2560]{2,1,0:T(8,128)} fusion(bf16[16,256,1280]{2,1,0:T(8,128)(2,1)} %get-tuple-element.17, bf16[2560,1280]{1,0:T(8,128)(2,1)} %param.17), kind=kOutput, calls=%fused_computation.46 | convolution fusion | flops 26843545600 | bytes 58982400 | tf_op jit(solution)/shard_map/blf,df->bld/dot_general | solution.py:86
  481.1 16.3 %fusion.95 = f32[16,256,2560]{2,1,0:T(8,128)} fusion(bf16[16,256,80]{1,2,0:T(8,128)(2,1)S(1)} %copy-done.10, bf16[2560,80]{0,1:T(8,128)(2,1)S(1)} %copy-done.18), kind=kOutput, calls=%fused_computation.113 | convolution fusion | flops 1677721600 | bytes 43008000 | tf_op jit(solution)/shard_map/blk,dk->bld/dot_general | solution.py:90
  497.4 17.3 %fusion.77 = f32[16,256,2560,1]{2,1,3,0:T(8,128)} fusion(bf16[16,256,4,40]{1,3,2,0:T(8,128)(2,1)S(1)} %copy-done.22, bf16[16,256,4,40]{1,3,2,0:T(8,128)(2,1)S(1)} %copy-done.20, bf16[2560,4,80]{0,2,1:T(8,128)(2,1)S(1)} %copy-done), kind=kOutput, calls=%fused_computation.92 | convolution fusion | flops 6716129280 | bytes 46202880 | tf_op jit(solution)/shard_map/blnk,dnk->bld/dot_general | solution.py:88
  514.7 16.2 %fusion.91 = f32[16,256,2560]{2,1,0:T(8,128)} fusion(bf16[16,256,40]{1,2,0:T(8,128)(2,1)S(1)} %copy-done.14, bf16[16,256,40]{1,2,0:T(8,128)(2,1)S(1)} %copy-done.13, bf16[2560,80]{0,1:T(8,128)(2,1)S(1)} %copy-done.16), kind=kOutput, calls=%fused_computation.109 | convolution fusion | flops 1679032320 | bytes 43008000 | tf_op jit(solution)/shard_map/blk,dk->bld/dot_general | solution.py:89
  531.0 67.6 %fusion.4 = bf16[16,256,2560]{2,1,0:T(8,128)(2,1)} fusion(f32[16,256,2560]{2,1,0:T(8,128)} %fusion.95, f32[16,256,2560]{2,1,0:T(8,128)} %fusion.91, f32[16,256,2560,1]{2,1,3,0:T(8,128)} %fusion.77, f32[16,256,2560]{2,1,0:T(8,128)} %fusion.29, bf16[16,256,1280]{2,1,0:T(8,128)(2,1)} %get-tuple-element.16, bf16[2560,1280]{1,0:T(8,128)(2,1)} %param.18), kind=kOutput, calls=%fused_computation.5 | convolution fusion | flops 26895974400 | bytes 205783040 | tf_op jit(solution)/shard_map/blf,df->bld/dot_general | solution.py:87
  598.6 0.0 reduce-scatter.3.cloned.1.call-start
  598.6 10.2 %convolution_bitcast_fusion.1 = f32[2560,80]{0,1:T(8,128)} fusion(bf16[16,256,2560]{2,1,0:T(8,128)(2,1)} %all-gather.3.cloned.1.call-done, bf16[16,256,40]{1,2,0:T(8,128)(2,1)S(1)} %copy-done.14, bf16[16,256,40]{1,2,0:T(8,128)(2,1)S(1)} %copy-done.13), kind=kOutput, calls=%fused_computation.79 | convolution fusion | flops 1679032320 | bytes 22446080 | tf_op jit(solution)/shard_map/bld,blk->dk/dot_general | solution.py:82
  608.9 9.8 %convolution_bitcast_fusion = f32[2560,80]{0,1:T(8,128)} fusion(bf16[16,256,80]{1,2,0:T(8,128)(2,1)S(1)} %copy-done.10, bf16[16,256,2560]{2,1,0:T(8,128)(2,1)} %all-gather.3.cloned.1.call-done), kind=kOutput, calls=%fused_computation.78 | convolution fusion | flops 1677721600 | bytes 22446080 | tf_op jit(solution)/shard_map/bld,blk->dk/dot_general | solution.py:83
  618.7 7.5 fusion.71
  626.2 17.1 %fusion.68 = f32[16,256,2560,1]{2,1,3,0:T(8,128)} fusion(bf16[16,80,4,256]{3,1,2,0:T(8,128)(2,1)S(1)} %fusion.71, bf16[4,80,2560]{2,1,0:T(8,128)(2,1)S(1)} %copy-done.30), kind=kOutput, calls=%fused_computation.83 | convolution fusion | flops 6710886400 | bytes 46202880 | tf_op jit(solution)/shard_map/crol,ole->cre/dot_general | solution.py:52
  643.3 36.8 %fusion.5 = bf16[16,256,2560]{2,1,0:T(8,128)(2,1)} fusion(f32[16,256,2560,1]{2,1,3,0:T(8,128)} %fusion.68, bf16[16,256,1280]{2,1,0:T(8,128)(2,1)} %get-tuple-element.18, bf16[1280,2560]{1,0:T(8,128)(2,1)} %param.19), kind=kOutput, calls=%fused_computation.7 | convolution fusion | flops 26864517120 | bytes 79953920 | tf_op jit(solution)/shard_map/blf,fd->bld/dot_general | solution.py:58
  680.2 13.0 %fusion.61 = bf16[4,80,2560]{2,1,0:T(8,128)(2,1)} fusion(bf16[16,256,2560]{2,1,0:T(8,128)(2,1)} %all-gather.5.cloned.1.call-done, bf16[16,80,4,256]{3,1,2,0:T(8,128)(2,1)} %copy-done.31), kind=kOutput, calls=%fused_computation.76 | convolution fusion | flops 6711705600 | bytes 25231360 | tf_op jit(solution)/shard_map/blnk,bld->nkd/dot_general | solution.py:72
  693.3 34.7 %bitcast_convert_fusion = bf16[1280,2560]{1,0:T(8,128)(2,1)} fusion(bf16[16,256,1280]{2,1,0:T(8,128)(2,1)} %get-tuple-element.18, bf16[16,256,2560]{2,1,0:T(8,128)(2,1)} %all-gather.5.cloned.1.call-done), kind=kOutput, calls=%fused_computation.28 | convolution fusion | flops 26846822400 | bytes 38010880 | tf_op jit(solution)/shard_map/blf,bld->fd/dot_general | solution.py:65
  728.0 34.4 %bitcast_convert_fusion.1 = bf16[2560,1280]{1,0:T(8,128)(2,1)} fusion(bf16[16,256,2560]{2,1,0:T(8,128)(2,1)S(1)} %bitcast.187, bf16[16,256,1280]{2,1,0:T(8,128)(2,1)} %get-tuple-element.16), kind=kOutput, calls=%fused_computation.29 | convolution fusion | flops 26846822400 | bytes 38010880 | tf_op jit(solution)/shard_map/bld,blf->df/dot_general | solution.py:69
  762.3 34.3 %bitcast_convert_fusion.2 = bf16[2560,1280]{1,0:T(8,128)(2,1)} fusion(bf16[16,256,2560]{2,1,0:T(8,128)(2,1)S(1)} %bitcast.187, bf16[16,256,1280]{2,1,0:T(8,128)(2,1)} %get-tuple-element.17), kind=kOutput, calls=%fused_computation.30 | convolution fusion | flops 26846822400 | bytes 38010880 | tf_op jit(solution)/shard_map/bld,blf->df/dot_general | solution.py:68
  796.7 12.9 %fusion.64 = bf16[2560,4,80]{0,2,1:T(8,128)(2,1)} fusion(bf16[16,256,2560]{2,1,0:T(8,128)(2,1)} %all-gather.3.cloned.1.call-done, bf16[16,256,4,40]{1,3,2,0:T(8,128)(2,1)S(1)} %copy-done.23, bf16[16,256,4,40]{1,3,2,0:T(8,128)(2,1)S(1)} %copy-done.21), kind=kOutput, calls=%fused_computation.77 | convolution fusion | flops 6716948480 | bytes 25231360 | tf_op jit(solution)/shard_map/bld,blnk->dnk/dot_general | solution.py:81
  809.6 4.2 fusion.49
  813.9 51.4 %all-reduce.2 = (f32[2560]{0:T(1024)}, bf16[2560,80]{0,1:T(8,128)(2,1)}, bf16[2560,80]{0,1:T(8,128)(2,1)}) all-reduce(f32[2560]{0:T(1024)S(1)} %get-tuple-element.10, f32[2560,80]{0,1:T(8,128)S(1)} %copy-done.11, f32[2560,80]{0,1:T(8,128)S(1)} %copy-done.12), channel_id=1, replica_groups=mesh['tp'=8] {'tp'}, use_global_device_ids=true, to_apply=%region_10.11 | all-reduce | flops 412160 | bytes 2478080 | tf_op jit(solution)/shard_map/psum | solution.py:93
  865.3 3.2 reduce-scatter.3.cloned.1.call-done
  868.5 7.2 fusion.46
  (98 shorter events, 0.3 us)
Async XLA Ops:
  7.2 126.9 %copy-start = (bf16[2560,4,80]{0,2,1:T(8,128)(2,1)S(1)}, bf16[2560,4,80]{0,2,1:T(8,128)(2,1)}, u32[]{:S(2)}) copy-start(bf16[2560,4,80]{0,2,1:T(8,128)(2,1)} %param.13) | copy-start | bytes 4915204
  7.2 113.5 %all-gather.3.cloned.1.call-start = ((), (), s32[]{:S(2)}) async-start(), calls=%async_computation.2 | async-start | bytes 23592960 | tf_op jit(solution)/shard_map/all_gather | solution.py:36
  7.2 5.6 copy-start.3
  9.6 2.6 copy-start.25
  9.6 111.2 %copy-start.15 = (bf16[2560,80]{0,1:T(8,128)(2,1)S(1)}, bf16[2560,80]{0,1:T(8,128)(2,1)}, u32[]{:S(2)}) copy-start(bf16[2560,80]{0,1:T(8,128)(2,1)} %param.14) | copy-start | bytes 1228804
  12.2 0.6 copy-start.27
  15.9 208.6 %all-gather.5.cloned.1.call-start = ((), (), s32[]{:S(2)}) async-start(), calls=%async_computation.4 | async-start | bytes 23592960 | tf_op jit(solution)/shard_map/all_gather | solution.py:63
  16.6 792.9 %reduce-scatter.5.cloned.1.call-start = ((), (), s32[]{:S(2)}) async-start(), calls=%async_computation.5 | async-start | bytes 23592960 | tf_op jit(solution)/shard_map/reduce_scatter | solution.py:92
  120.7 13.3 %copy-start.2 = (bf16[16,256,2560]{2,1,0:T(8,128)(2,1)S(1)}, bf16[16,256,2560]{2,1,0:T(8,128)(2,1)}, u32[]{:S(2)}) copy-start(bf16[16,256,2560]{2,1,0:T(8,128)(2,1)} %all-gather.3.cloned.1.call-done) | copy-start | bytes 62914564
  134.1 110.4 %copy-start.24 = (bf16[16,256,40]{1,2,0:T(8,128)(2,1)}, bf16[16,256,40]{1,2,0:T(8,128)(2,1)S(1)}, u32[]{:S(2)}) copy-start(bf16[16,256,40]{1,2,0:T(8,128)(2,1)S(1)} %get-tuple-element.28) | copy-start | bytes 983044
  142.7 4.9 copy-start.17
  154.0 82.2 %copy-start.5 = (bf16[16,256,80,1]{1,2,3,0:T(8,128)(2,1)}, bf16[16,256,80,1]{1,2,3,0:T(8,128)(2,1)S(1)}, u32[]{:S(2)}) copy-start(bf16[16,256,80,1]{1,2,3,0:T(8,128)(2,1)S(1)} %fusion.90) | copy-start | bytes 1966084
  236.3 8.2 copy-start.4
  236.3 8.2 copy-start.7
  236.3 8.2 copy-start.9
  270.4 33.5 %copy-start.32 = (f32[16,4,256]{2,1,0:T(4,128)}, f32[16,4,256]{2,1,0:T(4,128)S(1)}, u32[]{:S(2)}) copy-start(f32[16,4,256]{2,1,0:T(4,128)S(1)} %get-tuple-element.32) | copy-start | bytes 196612
  270.4 10.1 %copy-start.8 = (bf16[16,256,4,40]{1,3,2,0:T(8,128)(2,1)S(1)}, bf16[16,256,4,40]{1,3,2,0:T(8,128)(2,1)}, u32[]{:S(2)}) copy-start(bf16[16,256,4,40]{1,3,2,0:T(8,128)(2,1)} %get-tuple-element.21) | copy-start | bytes 3932164
  328.9 5.0 copy-start.19
  328.9 40.6 %slice-start = ((s8[20971520]{0:T(1024)(128)(4,1)}), s8[4194304]{0:T(1024)(128)(4,1)S(1)}, s32[]{:S(2)}) async-start(s8[20971520]{0:T(1024)(128)(4,1)} %bitcast.184), calls=%async_computation.6 | async-start | bytes 8388608
  335.0 34.6 %slice-start.1 = ((s8[20971520]{0:T(1024)(128)(4,1)}), s8[4194304]{0:T(1024)(128)(4,1)S(1)}, s32[]{:S(2)}) async-start(s8[20971520]{0:T(1024)(128)(4,1)} %bitcast.184), calls=%async_computation.7 | async-start | bytes 8388608
  335.0 34.6 %slice-start.2 = ((s8[20971520]{0:T(1024)(128)(4,1)}), s8[4194304]{0:T(1024)(128)(4,1)S(1)}, s32[]{:S(2)}) async-start(s8[20971520]{0:T(1024)(128)(4,1)} %bitcast.184), calls=%async_computation.8 | async-start | bytes 8388608
  335.0 34.6 %slice-start.3 = ((s8[20971520]{0:T(1024)(128)(4,1)}), s8[4194304]{0:T(1024)(128)(4,1)S(1)}, s32[]{:S(2)}) async-start(s8[20971520]{0:T(1024)(128)(4,1)} %bitcast.184), calls=%async_computation.9 | async-start | bytes 8388608
  335.0 34.6 %slice-start.4 = ((s8[20971520]{0:T(1024)(128)(4,1)}), s8[4194304]{0:T(1024)(128)(4,1)S(1)}, s32[]{:S(2)}) async-start(s8[20971520]{0:T(1024)(128)(4,1)} %bitcast.184), calls=%async_computation.10 | async-start | bytes 8388608
  445.4 35.6 %copy-start.10 = (bf16[16,256,80]{1,2,0:T(8,128)(2,1)S(1)}, bf16[16,256,80]{1,2,0:T(8,128)(2,1)}, u32[]{:S(2)}) copy-start(bf16[16,256,80]{1,2,0:T(8,128)(2,1)} %fusion.87) | copy-start | bytes 1966084
  445.4 35.6 %copy-start.18 = (bf16[2560,80]{0,1:T(8,128)(2,1)S(1)}, bf16[2560,80]{0,1:T(8,128)(2,1)}, u32[]{:S(2)}) copy-start(bf16[2560,80]{0,1:T(8,128)(2,1)} %param.15) | copy-start | bytes 1228804
  481.1 16.3 %copy-start.20 = (bf16[16,256,4,40]{1,3,2,0:T(8,128)(2,1)S(1)}, bf16[16,256,4,40]{1,3,2,0:T(8,128)(2,1)}, u32[]{:S(2)}) copy-start(bf16[16,256,4,40]{1,3,2,0:T(8,128)(2,1)} %get-tuple-element.19) | copy-start | bytes 3932164
  481.1 16.3 %copy-start.22 = (bf16[16,256,4,40]{1,3,2,0:T(8,128)(2,1)S(1)}, bf16[16,256,4,40]{1,3,2,0:T(8,128)(2,1)}, u32[]{:S(2)}) copy-start(bf16[16,256,4,40]{1,3,2,0:T(8,128)(2,1)} %get-tuple-element.20) | copy-start | bytes 3932164
  497.4 17.3 %copy-start.13 = (bf16[16,256,40]{1,2,0:T(8,128)(2,1)S(1)}, bf16[16,256,40]{1,2,0:T(8,128)(2,1)}, u32[]{:S(2)}) copy-start(bf16[16,256,40]{1,2,0:T(8,128)(2,1)} %get-tuple-element.25) | copy-start | bytes 983044
  497.4 17.3 %copy-start.14 = (bf16[16,256,40]{1,2,0:T(8,128)(2,1)S(1)}, bf16[16,256,40]{1,2,0:T(8,128)(2,1)}, u32[]{:S(2)}) copy-start(bf16[16,256,40]{1,2,0:T(8,128)(2,1)} %get-tuple-element.26) | copy-start | bytes 983044
  497.4 17.3 %copy-start.16 = (bf16[2560,80]{0,1:T(8,128)(2,1)S(1)}, bf16[2560,80]{0,1:T(8,128)(2,1)}, u32[]{:S(2)}) copy-start(bf16[2560,80]{0,1:T(8,128)(2,1)} %param.14) | copy-start | bytes 1228804
  598.6 269.9 %reduce-scatter.3.cloned.1.call-start = ((), (), s32[]{:S(2)}) async-start(), calls=%async_computation.3 | async-start | bytes 23592960 | tf_op jit(solution)/shard_map/reduce_scatter | solution.py:60
  608.9 9.8 %copy-start.6 = (bf16[16,256,80,1]{1,2,3,0:T(8,128)(2,1)S(1)}, bf16[16,256,80,1]{1,2,3,0:T(8,128)(2,1)}, u32[]{:S(2)}) copy-start(bf16[16,256,80,1]{1,2,3,0:T(8,128)(2,1)} %copy-done.5) | copy-start | bytes 1966084
  608.9 9.8 %copy-start.33 = (f32[16,4,256]{2,1,0:T(4,128)S(1)}, f32[16,4,256]{2,1,0:T(4,128)}, u32[]{:S(2)}) copy-start(f32[16,4,256]{2,1,0:T(4,128)} %copy-done.32) | copy-start | bytes 196612
  618.7 7.5 copy-start.30
  626.2 17.1 %copy-start.31 = (bf16[16,80,4,256]{3,1,2,0:T(8,128)(2,1)}, bf16[16,80,4,256]{3,1,2,0:T(8,128)(2,1)S(1)}, u32[]{:S(2)}) copy-start(bf16[16,80,4,256]{3,1,2,0:T(8,128)(2,1)S(1)} %fusion.71) | copy-start | bytes 7864324
  680.2 47.7 %slice-start.5 = ((s8[20971520]{0:T(1024)(128)(4,1)}), s8[4194304]{0:T(1024)(128)(4,1)S(1)}, s32[]{:S(2)}) async-start(s8[20971520]{0:T(1024)(128)(4,1)} %bitcast.186), calls=%async_computation.11 | async-start | bytes 8388608
  680.2 47.7 %slice-start.6 = ((s8[20971520]{0:T(1024)(128)(4,1)}), s8[4194304]{0:T(1024)(128)(4,1)S(1)}, s32[]{:S(2)}) async-start(s8[20971520]{0:T(1024)(128)(4,1)} %bitcast.186), calls=%async_computation.12 | async-start | bytes 8388608
  693.3 34.7 %slice-start.7 = ((s8[20971520]{0:T(1024)(128)(4,1)}), s8[4194304]{0:T(1024)(128)(4,1)S(1)}, s32[]{:S(2)}) async-start(s8[20971520]{0:T(1024)(128)(4,1)} %bitcast.186), calls=%async_computation.13 | async-start | bytes 8388608
  693.3 34.7 %slice-start.8 = ((s8[20971520]{0:T(1024)(128)(4,1)}), s8[4194304]{0:T(1024)(128)(4,1)S(1)}, s32[]{:S(2)}) async-start(s8[20971520]{0:T(1024)(128)(4,1)} %bitcast.186), calls=%async_computation.14 | async-start | bytes 8388608
  693.3 34.7 %slice-start.9 = ((s8[20971520]{0:T(1024)(128)(4,1)}), s8[4194304]{0:T(1024)(128)(4,1)S(1)}, s32[]{:S(2)}) async-start(s8[20971520]{0:T(1024)(128)(4,1)} %bitcast.186), calls=%async_computation.15 | async-start | bytes 8388608
  762.3 34.3 %copy-start.21 = (bf16[16,256,4,40]{1,3,2,0:T(8,128)(2,1)S(1)}, bf16[16,256,4,40]{1,3,2,0:T(8,128)(2,1)}, u32[]{:S(2)}) copy-start(bf16[16,256,4,40]{1,3,2,0:T(8,128)(2,1)} %get-tuple-element.19) | copy-start | bytes 3932164
  762.3 34.3 %copy-start.23 = (bf16[16,256,4,40]{1,3,2,0:T(8,128)(2,1)S(1)}, bf16[16,256,4,40]{1,3,2,0:T(8,128)(2,1)}, u32[]{:S(2)}) copy-start(bf16[16,256,4,40]{1,3,2,0:T(8,128)(2,1)} %get-tuple-element.20) | copy-start | bytes 3932164
  796.6 13.0 %copy-start.26 = (f32[16,32]{1,0:T(8,128)S(1)}, f32[16,32]{1,0:T(8,128)}, u32[]{:S(2)}) copy-start(f32[16,32]{1,0:T(8,128)} %copy-done.25) | copy-start | bytes 6148
  796.6 13.0 %copy-start.28 = (f32[16,32]{1,0:T(8,128)S(1)}, f32[16,32]{1,0:T(8,128)}, u32[]{:S(2)}) copy-start(f32[16,32]{1,0:T(8,128)} %copy-done.27) | copy-start | bytes 6148
  796.6 13.0 %copy-start.29 = (f32[2560]{0:T(1024)S(1)}, f32[2560]{0:T(1024)}, u32[]{:S(2)}) copy-start(f32[2560]{0:T(1024)} %param.12) | copy-start | bytes 30724
  796.7 17.2 %copy-start.11 = (f32[2560,80]{0,1:T(8,128)S(1)}, f32[2560,80]{0,1:T(8,128)}, u32[]{:S(2)}) copy-start(f32[2560,80]{0,1:T(8,128)} %convolution_bitcast_fusion.1) | copy-start | bytes 2457604
  796.7 17.2 %copy-start.12 = (f32[2560,80]{0,1:T(8,128)S(1)}, f32[2560,80]{0,1:T(8,128)}, u32[]{:S(2)}) copy-start(f32[2560,80]{0,1:T(8,128)} %convolution_bitcast_fusion) | copy-start | bytes 2457604
  868.5 7.2 copy-start.1
Sparse Core Ops, SparseCore 0:
  16.0 104.6 all-gather.2
  122.6 101.8 all-gather.4
  598.7 126.8 reduce-scatter.4
  729.0 139.4 reduce-scatter.2
where the time goes:
time: 885 us; the launch traced here: 883 us
  matrix products  589 us (67%)
  waiting for transfers between devices  178 us (20%)
  blocking collectives  51.4 us (6%)
  other arithmetic  48.6 us (5%)
  between operations  14.5 us (2%)
    all_gather x1, waiting for transfers between devices, layer_shard(): normed = lax.all_gather(normed_loc, 'tp', axis=1, tiled=True)  104 us
    all_gather x1, waiting for transfers between devices, layer_shard(): grad_full = lax.all_gather(grad_y_loc, 'tp', axis=1, tiled=True)  70.4 us
    dot_general x1, matrix products, layer_shard(): jnp.einsum('blf,df->bld', grad_up, w_up, preferred_element_type=jnp.float32)  67.6 us
    psum x1, blocking collectives, layer_shard(): grad_gain = lax.psum(jnp.sum(grad_normed_loc * x_hat, axis=(0, 1)), 'tp')  51.4 us
    dot_general x1, matrix products, layer_shard(): jnp.einsum('bld,fd->blf', grad_full, w_down, preferred_element_type=jnp.f...  44.2 us
    dot_general x1, matrix products, layer_shard(): jnp.einsum('blf,fd->bld', hidden, w_down, preferred_element_type=jnp.floa...  36.8 us
    dot_general x1, matrix products, layer_shard(): jnp.einsum('blf,df->bld', grad_gate, w_gate, preferred_element_type=jnp.f...  35.6 us
    dot_general x1, matrix products, layer_shard(): jnp.einsum('blf,bld->fd', hidden, grad_full, preferred_element_type=jnp.f...  34.7 us
  transfers between devices with their start and end apart: 4, of which 3 were waited for; matrix products, arithmetic and copies ran while one was open for 28% of the time, Pallas kernels for 0%

commit v1 on v0

v1 whole, which is shorter than its diff:
```python
import functools

import jax
import jax.numpy as jnp
from jax import lax
from jax.experimental import pallas as pl
from jax.experimental.pallas import tpu as pltpu
from jax.sharding import PartitionSpec as P

LN_EPS = 1e-6
ROPE_BASE = 10000.0
BF = jnp.bfloat16
F32 = jnp.float32
CHUNKS = 2
VMEM_LIMIT = 60 * 1024 * 1024
NT_DIMS = (((1,), (1,)), ((), ()))


def rope_tables(seq_len, head_dim):
    half_dim = head_dim // 2
    inv_freq = ROPE_BASE ** (-jnp.arange(half_dim, dtype=F32) * 2.0 / head_dim)
    angles = jnp.arange(seq_len, dtype=F32)[:, None] * inv_freq[None, :]
    return jnp.cos(angles).T, jnp.sin(angles).T


def rotate(values, cos_tab, sin_tab):
    half = values.shape[0] // 2
    first, second = values[:half], values[half:]
    return jnp.concatenate([first * cos_tab - second * sin_tab, second * cos_tab + first * sin_tab], axis=0)


def attn_fwd_kernel(heads, scale, qkv_ref, cos_ref, sin_ref, o_ref, rot_ref, stat_ref):
    hd = 2 * cos_ref.shape[0]
    cos, sin = cos_ref[...], sin_ref[...]
    seq = cos.shape[1]
    k_t = rotate(qkv_ref[0, heads * hd:(heads + 1) * hd], cos, sin)
    v_t = qkv_ref[0, (heads + 1) * hd:].astype(BF)
    rot_ref[0, heads * hd:(heads + 1) * hd] = k_t.astype(BF)
    rot_ref[0, (heads + 1) * hd:] = v_t
    k = k_t.T.astype(BF)
    causal = lax.broadcasted_iota(jnp.int32, (seq, seq), 0) <= lax.broadcasted_iota(jnp.int32, (seq, seq), 1)
    outs = []
    for n in range(heads):
        q_t = rotate(qkv_ref[0, n * hd:(n + 1) * hd], cos, sin).astype(BF)
        rot_ref[0, n * hd:(n + 1) * hd] = q_t
        scores = jnp.dot(k, q_t, preferred_element_type=F32) * scale
        scores = jnp.where(causal, scores, -1e30)
        top = jnp.max(scores, axis=0, keepdims=True)
        expd = jnp.exp(scores - top)
        inv = 1.0 / jnp.sum(expd, axis=0, keepdims=True)
        stat_ref[0, n:n + 1] = top
        stat_ref[0, heads + n:heads + n + 1] = inv
        probs = (expd * inv).astype(BF)
        outs.append(jnp.dot(v_t, probs, preferred_element_type=F32))
    o_ref[0] = jnp.concatenate(outs, axis=0).T.astype(BF)


def attn_bwd_kernel(heads, scale, rot_ref, do_ref, stat_ref, cos_ref, sin_ref, dqkv_ref):
    hd = 2 * cos_ref.shape[0]
    cos, sin = cos_ref[...], sin_ref[...]
    seq = cos.shape[1]
    k_t = rot_ref[0, heads * hd:(heads + 1) * hd]
    v_t = rot_ref[0, (heads + 1) * hd:]
    k = k_t.astype(F32).T.astype(BF)
    v = v_t.astype(F32).T.astype(BF)
    causal = lax.broadcasted_iota(jnp.int32, (seq, seq), 0) <= lax.broadcasted_iota(jnp.int32, (seq, seq), 1)
    grads = []
    dk_t = jnp.zeros((hd, seq), F32)
    dv_t = jnp.zeros((hd, seq), F32)
    for n in range(heads):
        q_t = rot_ref[0, n * hd:(n + 1) * hd]
        do_t = do_ref[0, n * hd:(n + 1) * hd]
        scores = jnp.dot(k, q_t, preferred_element_type=F32) * scale
        scores = jnp.where(causal, scores, -1e30)
        probs = jnp.exp(scores - stat_ref[0, n:n + 1]) * stat_ref[0, heads + n:heads + n + 1]
        dprobs = jnp.dot(v, do_t, preferred_element_type=F32)
        row_dot = jnp.sum(probs * dprobs, axis=0, keepdims=True)
        dscores = (probs * (dprobs - row_dot) * scale).astype(BF)
        grads.append(rotate(jnp.dot(k_t, dscores, preferred_element_type=F32), cos, -sin))
        dk_t += lax.dot_general(q_t, dscores, NT_DIMS, preferred_element_type=F32)
        dv_t += lax.dot_general(do_t, probs.astype(BF), NT_DIMS, preferred_element_type=F32)
    grads += [rotate(dk_t, cos, -sin), dv_t]
    dqkv_ref[0] = jnp.concatenate(grads, axis=0).T.astype(BF)


def attn_fwd(qkv_t, cos, sin, heads):
    batch, rows, seq = qkv_t.shape
    hd = rows // (heads + 2)
    block = lambda r, c: pl.BlockSpec((1, r, c), lambda b: (b, 0, 0))
    table = pl.BlockSpec(cos.shape, lambda b: (0, 0))
    return pl.pallas_call(
        functools.partial(attn_fwd_kernel, heads, hd ** -0.5),
        grid=(batch,),
        out_shape=(
            jax.ShapeDtypeStruct((batch, seq, heads * hd), BF),
            jax.ShapeDtypeStruct((batch, rows, seq), BF),
            jax.ShapeDtypeStruct((batch, 2 * heads, seq), F32),
        ),
        in_specs=[block(rows, seq), table, table],
        out_specs=(block(seq, heads * hd), block(rows, seq), block(2 * heads, seq)),
        compiler_params=pltpu.CompilerParams(vmem_limit_bytes=32 * 1024 * 1024),
        cost_estimate=pl.CostEstimate(flops=batch * 10_000_000_00, bytes_accessed=batch * rows * seq * 8, transcendentals=0),
        name="attn_fwd",
    )(qkv_t, cos, sin)


def attn_bwd(rot, do_t, stat, cos, sin, heads):
    batch, rows, seq = rot.shape
    hd = rows // (heads + 2)
    block = lambda r, c: pl.BlockSpec((1, r, c), lambda b: (b, 0, 0))
    table = pl.BlockSpec(cos.shape, lambda b: (0, 0))
    return pl.pallas_call(
        functools.partial(attn_bwd_kernel, heads, hd ** -0.5),
        grid=(batch,),
        out_shape=jax.ShapeDtypeStruct((batch, seq, rows), BF),
        in_specs=[block(rows, seq), block(heads * hd, seq), block(2 * heads, seq), table, table],
        out_specs=block(seq, rows),
        compiler_params=pltpu.CompilerParams(vmem_limit_bytes=32 * 1024 * 1024),
        cost_estimate=pl.CostEstimate(flops=batch * 20_000_000_00, bytes_accessed=batch * rows * seq * 6, transcendentals=0),
        name="attn_bwd",
    )(rot, do_t, stat, cos, sin)


def pair_matmul_kernel(num, trans, tiles, *refs):
    a_hbm, b_refs, out_ref = refs[:num], refs[num:2 * num], refs[2 * num]
    a_vmem = refs[2 * num + 1:3 * num + 1]
    send_buf, recv_buf, a_sem, send_sem, recv_sem = refs[3 * num + 1:]
    step = pl.program_id(0)
    me = lax.axis_index("tp")
    core = lax.rem(me, 2)
    partner = me + 1 - 2 * core
    chips = a_vmem[0].shape[1]

    def load(half, which, chip):
        parity = 1 - core if half == 0 else core
        return pltpu.make_async_copy(a_hbm[which].at[:, chip, parity], a_vmem[which].at[half, chip], a_sem.at[half, which, chip])

    def exchange(tile):
        return pltpu.make_async_remote_copy(
            src_ref=send_buf.at[tile], dst_ref=recv_buf.at[tile], send_sem=send_sem.at[tile], recv_sem=recv_sem.at[tile],
            device_id=(partner,), device_id_type=pl.DeviceIdType.MESH)

    def product(half, rows):
        total = None
        for which in range(num):
            lhs = a_vmem[which][half, rows]
            lhs = lhs.reshape(-1, lhs.shape[-1])
            rhs = b_refs[which][...]
            term = lax.dot_general(lhs, rhs, NT_DIMS, preferred_element_type=F32) if trans[which] else jnp.dot(lhs, rhs, preferred_element_type=F32)
            total = term if total is None else total + term
        return total

    group = 2
    shape = (group,) + send_buf.shape[2:]

    @pl.when(step == 0)
    def _():
        for half in range(2):
            for which in range(num):
                for chip in range(chips):
                    load(half, which, chip).start()
        barrier = pltpu.get_barrier_semaphore()
        pl.semaphore_signal(barrier, inc=1, device_id=(partner,), device_id_type=pl.DeviceIdType.MESH)
        pl.semaphore_wait(barrier, 1)
        for which in range(num):
            for chip in range(chips):
                load(0, which, chip).wait()

    for tile in range(tiles):
        @pl.when(step == tile + 1)
        def _():
            exchange(tile).start()

    @pl.when(step == tiles)
    def _():
        for which in range(num):
            for chip in range(chips):
                load(1, which, chip).wait()

    for tile in range(tiles):
        @pl.when(step == tile + tiles)
        def _():
            exchange(tile).wait_recv()

    @pl.when(step < tiles)
    def _():
        @pl.loop(0, chips // group)
        def _(g):
            rows = pl.ds(g * group, group)
            send_buf[step, rows] = product(0, rows).astype(BF).reshape(shape)

    @pl.when(step >= tiles)
    def _():
        @pl.loop(0, chips // group)
        def _(g):
            rows = pl.ds(g * group, group)
            arrived = recv_buf[step - tiles, rows].reshape(-1, shape[-1])
            out_ref[rows] = (product(1, rows) + arrived.astype(F32)).astype(BF).reshape(shape)

    @pl.when(step == 2 * tiles - 1)
    def _():
        for tile in range(tiles):
            exchange(tile).wait_send()


def pair_matmul(lhs, rhs, trans, collective_id, name, tile=512):
    num = len(lhs)
    batch, seq = lhs[0].shape[:2]
    chips, local = 4, seq // 8
    lhs = [a.reshape(batch, chips, 2, local, a.shape[-1]) for a in lhs]
    width = rhs[0].shape[0] if trans[0] else rhs[0].shape[1]
    tiles = width // tile
    in_specs = [pl.BlockSpec(memory_space=pl.ANY)] * num
    for b, t in zip(rhs, trans):
        if t:
            in_specs.append(pl.BlockSpec((tile, b.shape[1]), lambda i: (lax.rem(i, tiles), 0)))
        else:
            in_specs.append(pl.BlockSpec((b.shape[0], tile), lambda i: (0, lax.rem(i, tiles))))
    depth = sum(a.shape[-1] for a in lhs)
    return pl.pallas_call(
        functools.partial(pair_matmul_kernel, num, trans, tiles),
        grid=(2 * tiles,),
        out_shape=jax.ShapeDtypeStruct((chips, batch, local, width), BF),
        in_specs=in_specs,
        out_specs=pl.BlockSpec((chips, batch, local, tile), lambda i: (0, 0, 0, lax.max(i - tiles, 0))),
        scratch_shapes=[pltpu.VMEM((2, chips, batch, local, a.shape[-1]), BF) for a in lhs] + [
            pltpu.VMEM((tiles, chips, batch, local, tile), BF),
            pltpu.VMEM((tiles, chips, batch, local, tile), BF),
            pltpu.SemaphoreType.DMA((2, num, chips)),
            pltpu.SemaphoreType.DMA((tiles,)),
            pltpu.SemaphoreType.DMA((tiles,)),
        ],
        compiler_params=pltpu.CompilerParams(collective_id=collective_id, has_side_effects=True, vmem_limit_bytes=VMEM_LIMIT),
        cost_estimate=pl.CostEstimate(flops=2 * batch * seq * width * depth, bytes_accessed=2 * depth * (batch * seq + width), transcendentals=0),
        name=name,
    )(*lhs, *rhs)


def solution(mesh):
    group_size = mesh.shape["tp"]
    same_core = [[c + 2 * j for j in range(group_size // 2)] for c in range(2)]

    def layer_shard(x_loc, grad_y_loc, ln_gain, w_query, w_key, w_value, w_out, w_gate, w_up, w_down):
        head_dim = w_key.shape[1]
        heads = w_query.shape[1]
        width = x_loc.shape[2]
        seq_len = x_loc.shape[1] * group_size
        rows = x_loc.shape[0] // CHUNKS
        cos_tab, sin_tab = rope_tables(seq_len, head_dim)
        w_qkv_t = jnp.concatenate([w_query.transpose(1, 2, 0).reshape(heads * head_dim, width), w_key.T, w_value.T], axis=0)
        w_out_2d = w_out.reshape(heads * head_dim, width)

        def normalize(x):
            residual = x.astype(F32)
            centered = residual - jnp.mean(residual, axis=-1, keepdims=True)
            inv_std = lax.rsqrt(jnp.mean(centered * centered, axis=-1, keepdims=True) + LN_EPS)
            return residual, centered * inv_std, inv_std

        xs = [x_loc[c * rows:(c + 1) * rows] for c in range(CHUNKS)]
        dys = [grad_y_loc[c * rows:(c + 1) * rows] for c in range(CHUNKS)]
        sums = {k: 0.0 for k in ("qkv", "out", "gate", "up", "down")}
        ys, dhs = [], []
        saved = []
        for c in range(CHUNKS):
            normed_loc = (ln_gain * normalize(xs[c])[1]).astype(BF)
            normed = lax.all_gather(normed_loc, "tp", axis=1, tiled=True)
            grad = lax.all_gather(dys[c], "tp", axis=1, tiled=True)
            qkv_t = jnp.einsum("kd,bld->bkl", w_qkv_t, normed, preferred_element_type=F32)
            attn, rot, stat = attn_fwd(qkv_t, cos_tab, sin_tab, heads)
            gate_pre = jnp.einsum("bld,df->blf", normed, w_gate, preferred_element_type=F32)
            up_pre = jnp.einsum("bld,df->blf", normed, w_up, preferred_element_type=F32)
            gate_sig = jax.nn.sigmoid(gate_pre)
            gate_act = gate_pre * gate_sig
            hidden = (gate_act * up_pre).astype(BF)
            branch = pair_matmul([hidden, attn], [w_down, w_out_2d], (False, False), 1, "branch_mm")
            ys.append(lax.psum_scatter(branch, "tp", scatter_dimension=0, tiled=False, axis_index_groups=same_core))

            do_t = jnp.einsum("kd,bld->bkl", w_out_2d, grad, preferred_element_type=F32).astype(BF)
            grad_hidden = jnp.einsum("bld,fd->blf", grad, w_down, preferred_element_type=F32)
            grad_gate = (grad_hidden * up_pre * gate_sig * (1.0 + gate_pre * (1.0 - gate_sig))).astype(BF)
            grad_up = (grad_hidden * gate_act).astype(BF)
            dqkv = attn_bwd(rot, do_t, stat, cos_tab, sin_tab, heads)
            dh = pair_matmul([grad_gate, grad_up, dqkv], [w_gate, w_up, w_qkv_t], (True, True, False), 2, "dh_mm")
            dhs.append(lax.psum_scatter(dh, "tp", scatter_dimension=0, tiled=False, axis_index_groups=same_core))
            saved.append((normed, grad, hidden, attn, grad_gate, grad_up, dqkv))

        total = lambda spec, i, j: sum(jnp.einsum(spec, s[i], s[j], preferred_element_type=F32) for s in saved)
        dw_qkv = total("blk,bld->kd", 6, 0)
        dw_kv = lax.psum(dw_qkv[heads * head_dim:], "tp")
        dw_query = dw_qkv[:heads * head_dim].reshape(heads, head_dim, width).transpose(2, 0, 1)
        dw_out = total("blk,bld->kd", 3, 1).reshape(heads, head_dim, width)
        dw_down = total("blf,bld->fd", 2, 1)
        dw_gate = total("bld,blf->df", 0, 4)
        dw_up = total("bld,blf->df", 0, 5)

        y_parts, dx_parts = [], []
        gain_sum = 0.0
        for c in range(CHUNKS):
            residual, x_hat, inv_std = normalize(xs[c])
            y_parts.append((residual + ys[c].astype(F32)).astype(BF))
            dh = dhs[c].astype(F32)
            gain_sum += jnp.sum(dh * x_hat, axis=(0, 1))
            grad_hat = dh * ln_gain
            dx = inv_std * (grad_hat - jnp.mean(grad_hat, axis=-1, keepdims=True) - x_hat * jnp.mean(grad_hat * x_hat, axis=-1, keepdims=True)) + dys[c].astype(F32)
            dx_parts.append(dx.astype(BF))
        return (
            jnp.concatenate(y_parts, axis=0),
            jnp.concatenate(dx_parts, axis=0),
            lax.psum(gain_sum, "tp"),
            dw_query.astype(BF),
            dw_kv[:head_dim].T.astype(BF),
            dw_kv[head_dim:].T.astype(BF),
            dw_out.astype(BF),
            dw_gate.astype(BF),
            dw_up.astype(BF),
            dw_down.astype(BF),
        )

    act_spec = P(None, "tp", None)
    weight_specs = (P(), P(None, "tp", None), P(), P(), P("tp", None, None), P(None, "tp"), P(None, "tp"), P("tp", None))
    return jax.shard_map(layer_shard, mesh=mesh, in_specs=(act_spec, act_spec) + weight_specs, out_specs=(act_spec, act_spec) + weight_specs, check_vma=False)
```

time: 885 us -> 726 us (0.82)
  matrix products: 589 us -> 308 us
  Pallas kernels: 0 us -> 193 us
  waiting for transfers between devices: 178 us -> 131 us
  other arithmetic: 48.6 us -> 21.4 us
  blocking collectives: 51.4 us -> 36.4 us
  local copies, waits for them, and re-layouts: 0.8 us -> 12.1 us
    dot_general x27 -> x20, matrix products: 589 us -> 308 us  [the longest x10 155 us: layer_shard(): jnp.einsum(spec, s[i], s[j], preferred_element_type=F32)]
    pallas_call x0 -> x8, Pallas kernels: none -> 193 us  [the longest x4 143 us: pair_matmul(): pl.pallas_call(functools.partial(pair_matmul_kernel, num, trans, tiles),...]
    all_gather x1 -> x2, waiting for transfers between devices: 70.4 us -> 38.2 us  [layer_shard(): grad = lax.all_gather(dys[c], 'tp', axis=1, tiled=True)]
    sub x1 -> x0, other arithmetic: 17.8 us -> none  [layer_shard(): attn_probs = jax.nn.softmax(jnp.where(causal, scores, -1e+30), axis=-1)]
    psum x1, blocking collectives: 51.4 us -> 36.4 us  [layer_shard(): lax.psum(gain_sum, 'tp')]
    all_gather x1 -> x2, waiting for transfers between devices: 104 us -> 91.1 us  [layer_shard(): normed = lax.all_gather(normed_loc, 'tp', axis=1, tiled=True)]
    another operation x4 -> x0, other arithmetic: 11.1 us -> none
  transfers between devices with their start and end apart: 4 -> 8, of which waited for: 3 -> 3; matrix products, arithmetic and copies ran while one was open for 28% -> 45% of each run, Pallas kernels for 0% -> 27%
where the time goes in v1:
time: 726 us; the launch traced here: 718 us
  matrix products  308 us (42%)
  Pallas kernels  193 us (27%)
  waiting for transfers between devices  131 us (18%)
  blocking collectives  36.4 us (5%)
  other arithmetic  21.4 us (3%)
  between operations  15.3 us (2%)
  local copies, waits for them, and re-layouts  12.1 us (2%)
    dot_general x10, matrix products, layer_shard(): jnp.einsum(spec, s[i], s[j], preferred_element_type=F32)  155 us
    pallas_call x4, Pallas kernels, pair_matmul(): pl.pallas_call(functools.partial(pair_matmul_kernel, num, trans, tiles),...  143 us
    all_gather x2, waiting for transfers between devices, layer_shard(): normed = lax.all_gather(normed_loc, 'tp', axis=1, tiled=True)  91.1 us
    dot_general x2, matrix products, layer_shard(): jnp.einsum('bld,fd->blf', grad, w_down, preferred_element_type=F32)  52.3 us
    all_gather x2, waiting for transfers between devices, layer_shard(): grad = lax.all_gather(dys[c], 'tp', axis=1, tiled=True)  38.2 us
    psum x1, blocking collectives, layer_shard(): lax.psum(gain_sum, 'tp')  36.4 us
    dot_general x2, matrix products, layer_shard(): jnp.einsum('bld,df->blf', normed, w_gate, preferred_element_type=F32)  35.8 us
    dot_general x2, matrix products, layer_shard(): up_pre = jnp.einsum('bld,df->blf', normed, w_up, preferred_element_type=F32)  32.3 us
  transfers between devices with their start and end apart: 8, of which 3 were waited for; matrix products, arithmetic and copies ran while one was open for 45% of the time, Pallas kernels for 27%

profile of v1, /device:TPU:0, one launch (start us, length us, event | category | flops | bytes accessed | tf_op | source)
XLA Modules:
  0.0 717.5 jit_solution(4460940150575143989)
XLA Ops:
  7.2 2.3 convert_reduce_fusion.1
  9.6 2.5 fusion.44
  12.1 2.3 fusion.39
  15.3 3.4 fusion.65
  19.7 1.6 pad_maximum_fusion.2.refs_5_
  21.3 53.6 %all-gather.5.cloned.1.call-done = bf16[8,256,2560]{2,1,0:T(8,128)(2,1)} async-done(((bf16[8,32,2560]{2,1,0:T(8,128)(2,1)}), bf16[8,256,2560]{2,1,0:T(8,128)(2,1)}) %all-gather.5.cloned.1.call-update) | async-done | bytes 10485776 | tf_op jit(solution)/shard_map/all_gather | solution.py:266
  74.9 8.0 %fusion.55.qkv_ref = f32[8,480,256]{2,1,0:T(8,128)S(1)} fusion(bf16[8,256,2560]{2,1,0:T(8,128)(2,1)} %all-gather.5.cloned.1.call-done, bf16[80,2560]{1,0:T(8,128)(2,1)S(1)} %bitcast.159, bf16[80,2560]{1,0:T(8,128)(2,1)S(1)} %bitcast.162, bf16[320,2560]{1,0:T(8,128)(2,1)S(1)} %bitcast.156), kind=kOutput, calls=%fused_computation.83 | convolution fusion | flops 5040537600 | bytes 16875520 | tf_op jit(solution)/shard_map/kd,bld->bkl/dot_general | solution.py:268
  82.9 12.0 %attn_fwd.2 = (bf16[8,256,320]{2,1,0:T(8,128)(2,1)S(1)}, bf16[8,480,256]{2,1,0:T(8,128)(2,1)S(1)}, f32[8,8,256]{2,1,0:T(8,128)S(1)}) custom-call(f32[8,480,256]{2,1,0:T(8,128)S(1)} %fusion.55.qkv_ref, f32[40,256]{1,0:T(8,128)S(1)} %get-tuple-element.53.cos_ref, f32[40,256]{1,0:T(8,128)S(1)} %get-tuple-element.52.sin_ref), custom_call_target="tpu_custom_call" | custom-call | flops 8000000000 | bytes 7864320 | tf_op jit(solution)/shard_map/attn_fwd/pallas_call | solution.py:91
  94.8 1.2 copy-done.2
  96.0 1.3 copy-done.7
  97.3 37.5 %all-gather.7.cloned.1.call-done = bf16[8,256,2560]{2,1,0:T(8,128)(2,1)} async-done(((bf16[8,32,2560]{2,1,0:T(8,128)(2,1)}), bf16[8,256,2560]{2,1,0:T(8,128)(2,1)}) %all-gather.7.cloned.1.call-update) | async-done | bytes 10485776 | tf_op jit(solution)/shard_map/all_gather | solution.py:266
  134.7 8.5 %fusion.58.qkv_ref = f32[8,480,256]{2,1,0:T(8,128)S(1)} fusion(bf16[8,256,2560]{2,1,0:T(8,128)(2,1)} %all-gather.7.cloned.1.call-done, bf16[80,2560]{1,0:T(8,128)(2,1)S(1)} %bitcast.160, bf16[80,2560]{1,0:T(8,128)(2,1)S(1)} %bitcast.163, bf16[320,2560]{1,0:T(8,128)(2,1)} %bitcast.154), kind=kOutput, calls=%fused_computation.84 | convolution fusion | flops 5040537600 | bytes 16875520 | tf_op jit(solution)/shard_map/kd,bld->bkl/dot_general | solution.py:268
  143.2 11.9 %attn_fwd.3 = (bf16[8,256,320]{2,1,0:T(8,128)(2,1)S(1)}, bf16[8,480,256]{2,1,0:T(8,128)(2,1)S(1)}, f32[8,8,256]{2,1,0:T(8,128)S(1)}) custom-call(f32[8,480,256]{2,1,0:T(8,128)S(1)} %fusion.58.qkv_ref, f32[40,256]{1,0:T(8,128)S(1)} %get-tuple-element.53.cos_ref, f32[40,256]{1,0:T(8,128)S(1)} %get-tuple-element.52.sin_ref), custom_call_target="tpu_custom_call" | custom-call | flops 8000000000 | bytes 7864320 | tf_op jit(solution)/shard_map/attn_fwd/pallas_call | solution.py:91
  155.2 1.1 copy-done.4
  156.3 38.2 %all-gather.9.cloned.1.call-done = bf16[8,256,2560]{2,1,0:T(8,128)(2,1)} async-done(((bf16[8,32,2560]{2,1,0:T(8,128)(2,1)}), bf16[8,256,2560]{2,1,0:T(8,128)(2,1)}) %all-gather.9.cloned.1.call-update) | async-done | bytes 10485776 | tf_op jit(solution)/shard_map/all_gather | solution.py:267
  194.6 8.1 %fusion.61.do_ref = bf16[8,320,256]{2,1,0:T(8,128)(2,1)S(1)} fusion(bf16[8,256,2560]{2,1,0:T(8,128)(2,1)} %all-gather.9.cloned.1.call-done, bf16[320,2560,1]{1,0,2:T(8,128)(2,1)} %bitcast.174), kind=kOutput, calls=%fused_computation.87 | convolution fusion | flops 3356098560 | bytes 13434880 | tf_op jit(solution)/shard_map/kd,bld->bkl/dot_general | solution.py:278
  202.8 13.5 %attn_bwd.2 = bf16[8,256,480]{2,1,0:T(8,128)(2,1)S(1)} custom-call(bf16[8,480,256]{2,1,0:T(8,128)(2,1)S(1)} %copy-done.8, bf16[8,320,256]{2,1,0:T(8,128)(2,1)S(1)} %fusion.61.do_ref, f32[8,8,256]{2,1,0:T(8,128)S(1)} %get-tuple-element.19.stat_ref, f32[40,256]{1,0:T(8,128)S(1)} %get-tuple-element.53.cos_ref, f32[40,256]{1,0:T(8,128)S(1)} %get-tuple-element.52.sin_ref), custom_call_target="tpu_custom_call" | custom-call | flops 16000000000 | bytes 5898240 | tf_op jit(solution)/shard_map/attn_bwd/pallas_call | solution.py:112
  216.4 16.4 %fusion.15 = f32[8,256,1280]{2,1,0:T(8,128)} fusion(bf16[8,256,2560]{2,1,0:T(8,128)(2,1)S(1)} %bitcast.165, bf16[2560,1280]{1,0:T(8,128)(2,1)S(1)} %bitcast.169), kind=kOutput, calls=%fused_computation.26 | convolution fusion | flops 13421772800 | bytes 27525120 | tf_op jit(solution)/shard_map/bld,df->blf/dot_general | solution.py:270
  232.8 16.1 %fusion.11 = f32[8,256,1280]{2,1,0:T(8,128)} fusion(bf16[8,256,2560]{2,1,0:T(8,128)(2,1)S(1)} %bitcast.165, bf16[2560,1280]{1,0:T(8,128)(2,1)S(1)} %bitcast.171), kind=kOutput, calls=%fused_computation.22 | convolution fusion | flops 13421772800 | bytes 27525120 | tf_op jit(solution)/shard_map/bld,df->blf/dot_general | solution.py:271
  248.9 26.1 %multiply_convert_fusion.2 = (bf16[8,256,1280]{2,1,0:T(8,128)(2,1)}, bf16[8,256,1280]{2,1,0:T(8,128)(2,1)}, bf16[8,256,1280]{2,1,0:T(8,128)(2,1)}) fusion(f32[8,256,1280]{2,1,0:T(8,128)} %fusion.15, f32[8,256,1280]{2,1,0:T(8,128)} %fusion.11, bf16[8,256,2560]{2,1,0:T(8,128)(2,1)} %all-gather.9.cloned.1.call-done, bf16[1280,2560]{1,0:T(8,128)(2,1)} %refs_2_.3), kind=kOutput, calls=%fused_computation.8 | convolution fusion | flops 13461094400 | bytes 53739520 | tf_op jit(solution)/shard_map/bld,fd->blf/dot_general | solution.py:279
  274.9 43.8 %dh_mm.2 = bf16[4,8,32,2560]{3,2,1,0:T(8,128)(2,1)} custom-call(bf16[8,4,2,32,1280]{4,3,2,1,0:T(8,128)(2,1)} %bitcast.180, bf16[8,4,2,32,1280]{4,3,2,1,0:T(8,128)(2,1)} %bitcast.179, bf16[8,4,2,32,480]{4,3,2,1,0:T(8,128)(2,1)} %bitcast.146, bf16[2560,1280]{1,0:T(8,128)(2,1)} %refs_3_.3, bf16[2560,1280]{1,0:T(8,128)(2,1)} %refs_4_.3, ...), custom_call_target="tpu_custom_call" | custom-call | flops 31876710400 | bytes 28016640 | tf_op jit(solution)/shard_map/dh_mm/pallas_call | solution.py:220
  318.8 19.4 %fusion.13 = f32[8,256,1280]{2,1,0:T(8,128)} fusion(bf16[8,256,2560]{2,1,0:T(8,128)(2,1)} %all-gather.7.cloned.1.call-done, bf16[2560,1280]{1,0:T(8,128)(2,1)} %refs_3_.3), kind=kOutput, calls=%fused_computation.24 | convolution fusion | flops 13421772800 | bytes 27525120 | tf_op jit(solution)/shard_map/bld,df->blf/dot_general | solution.py:270
  338.3 8.1 %fusion.62.do_ref = bf16[8,320,256]{2,1,0:T(8,128)(2,1)S(1)} fusion(bf16[8,256,2560]{2,1,0:T(8,128)(2,1)} %all-gather.11.cloned.1.call-done, bf16[320,2560,1]{1,0,2:T(8,128)(2,1)} %bitcast.175), kind=kOutput, calls=%fused_computation.88 | convolution fusion | flops 3356098560 | bytes 13434880 | tf_op jit(solution)/shard_map/kd,bld->bkl/dot_general | solution.py:278
  346.4 13.5 %attn_bwd.3 = bf16[8,256,480]{2,1,0:T(8,128)(2,1)S(1)} custom-call(bf16[8,480,256]{2,1,0:T(8,128)(2,1)S(1)} %get-tuple-element.20.rot_ref, bf16[8,320,256]{2,1,0:T(8,128)(2,1)S(1)} %fusion.62.do_ref, f32[8,8,256]{2,1,0:T(8,128)S(1)} %get-tuple-element.21.stat_ref, f32[40,256]{1,0:T(8,128)S(1)} %get-tuple-element.53.cos_ref, ...), custom_call_target="tpu_custom_call" | custom-call | flops 16000000000 | bytes 5898240 | tf_op jit(solution)/shard_map/attn_bwd/pallas_call | solution.py:112
  360.0 1.3 copy-done
  361.3 16.1 %fusion.9 = f32[8,256,1280]{2,1,0:T(8,128)} fusion(bf16[8,256,2560]{2,1,0:T(8,128)(2,1)S(1)} %bitcast.150, bf16[2560,1280]{1,0:T(8,128)(2,1)S(1)} %bitcast.173), kind=kOutput, calls=%fused_computation.20 | convolution fusion | flops 13421772800 | bytes 27525120 | tf_op jit(solution)/shard_map/bld,df->blf/dot_general | solution.py:271
  377.4 26.2 %multiply_convert_fusion = (bf16[8,256,1280]{2,1,0:T(8,128)(2,1)}, bf16[8,256,1280]{2,1,0:T(8,128)(2,1)}, bf16[8,256,1280]{2,1,0:T(8,128)(2,1)}) fusion(f32[8,256,1280]{2,1,0:T(8,128)} %fusion.13, f32[8,256,1280]{2,1,0:T(8,128)} %fusion.9, bf16[8,256,2560]{2,1,0:T(8,128)(2,1)} %all-gather.11.cloned.1.call-done, bf16[1280,2560]{1,0:T(8,128)(2,1)} %refs_2_.3), kind=kOutput, calls=%fused_computation.6 | convolution fusion | flops 13461094400 | bytes 53739520 | tf_op jit(solution)/shard_map/bld,fd->blf/dot_general | solution.py:279
  403.6 43.4 %dh_mm.3 = bf16[4,8,32,2560]{3,2,1,0:T(8,128)(2,1)} custom-call(bf16[8,4,2,32,1280]{4,3,2,1,0:T(8,128)(2,1)} %bitcast.183, bf16[8,4,2,32,1280]{4,3,2,1,0:T(8,128)(2,1)} %bitcast.182, bf16[8,4,2,32,480]{4,3,2,1,0:T(8,128)(2,1)} %bitcast.143, bf16[2560,1280]{1,0:T(8,128)(2,1)} %refs_3_.3, bf16[2560,1280]{1,0:T(8,128)(2,1)} %refs_4_.3, ...), custom_call_target="tpu_custom_call" | custom-call | flops 31876710400 | bytes 28016640 | tf_op jit(solution)/shard_map/dh_mm/pallas_call | solution.py:220
  447.1 27.7 %branch_mm.3 = bf16[4,8,32,2560]{3,2,1,0:T(8,128)(2,1)} custom-call(bf16[8,4,2,32,1280]{4,3,2,1,0:T(8,128)(2,1)} %bitcast.181, bf16[8,4,2,32,320]{4,3,2,1,0:T(8,128)(2,1)} %bitcast.145, bf16[1280,2560]{1,0:T(8,128)(2,1)} %refs_2_.3, bf16[320,2560]{1,0:T(8,128)(2,1)} %bitcast.176), custom_call_target="tpu_custom_call" | custom-call | flops 16777216000 | bytes 14745600 | tf_op jit(solution)/shard_map/branch_mm/pallas_call | solution.py:220
  474.9 9.2 %fusion.66 = f32[480,2560,1]{1,0,2:T(8,128)S(1)} fusion(bf16[8,256,480]{2,1,0:T(8,128)(2,1)} %copy-done.6, bf16[8,256,2560]{2,1,0:T(8,128)(2,1)} %all-gather.5.cloned.1.call-done), kind=kOutput, calls=%fused_computation.104 | convolution fusion | flops 5033164800 | bytes 17367040 | tf_op jit(solution)/shard_map/blk,bld->kd/dot_general | solution.py:287
  484.1 8.2 %bitcast_add_fusion.3 = f32[480,2560]{1,0:T(8,128)S(1)} fusion(f32[480,2560,1]{1,0,2:T(8,128)S(1)} %fusion.66, bf16[8,256,480]{2,1,0:T(8,128)(2,1)S(1)} %copy-done.1, bf16[8,256,2560]{2,1,0:T(8,128)(2,1)} %all-gather.7.cloned.1.call-done), kind=kOutput, calls=%fused_computation.28 | convolution fusion | flops 5034393600 | bytes 22282240 | tf_op jit(solution)/shard_map/blk,bld->kd/dot_general | solution.py:287
  492.3 1.3 slice.36
  493.5 1.3 slice.58
  494.9 27.7 %branch_mm.2 = bf16[4,8,32,2560]{3,2,1,0:T(8,128)(2,1)} custom-call(bf16[8,4,2,32,1280]{4,3,2,1,0:T(8,128)(2,1)} %bitcast.178, bf16[8,4,2,32,320]{4,3,2,1,0:T(8,128)(2,1)} %bitcast.144, bf16[1280,2560]{1,0:T(8,128)(2,1)} %refs_2_.3, bf16[320,2560]{1,0:T(8,128)(2,1)} %bitcast.177), custom_call_target="tpu_custom_call" | custom-call | flops 16777216000 | bytes 14745600 | tf_op jit(solution)/shard_map/branch_mm/pallas_call | solution.py:220
  522.6 19.8 %fusion.67 = f32[2560,1280,1]{1,0,2:T(8,128)} fusion(bf16[8,256,2560]{2,1,0:T(8,128)(2,1)} %all-gather.5.cloned.1.call-done, bf16[8,256,1280]{2,1,0:T(8,128)(2,1)} %get-tuple-element.37), kind=kOutput, calls=%fused_computation.105 | convolution fusion | flops 13421772800 | bytes 28835840 | tf_op jit(solution)/shard_map/bld,blf->df/dot_general | solution.py:287
  542.5 20.1 %fusion.68 = f32[2560,1280,1]{1,0,2:T(8,128)} fusion(bf16[8,256,2560]{2,1,0:T(8,128)(2,1)S(1)} %bitcast.167, bf16[8,256,1280]{2,1,0:T(8,128)(2,1)} %get-tuple-element.36), kind=kOutput, calls=%fused_computation.106 | convolution fusion | flops 13421772800 | bytes 28835840 | tf_op jit(solution)/shard_map/bld,blf->df/dot_general | solution.py:287
  562.6 18.6 %fusion.69 = f32[1280,2560,1]{1,0,2:T(8,128)} fusion(bf16[8,256,1280]{2,1,0:T(8,128)(2,1)} %get-tuple-element.38, bf16[8,256,2560]{2,1,0:T(8,128)(2,1)S(1)} %bitcast.148), kind=kOutput, calls=%fused_computation.107 | convolution fusion | flops 13421772800 | bytes 28835840 | tf_op jit(solution)/shard_map/blf,bld->fd/dot_general | solution.py:287
  581.2 22.0 %fusion.2 = bf16[2560,1280]{1,0:T(8,128)(2,1)} fusion(f32[2560,1280,1]{1,0,2:T(8,128)} %fusion.67, bf16[8,256,2560]{2,1,0:T(8,128)(2,1)} %all-gather.7.cloned.1.call-done, bf16[8,256,1280]{2,1,0:T(8,128)(2,1)} %get-tuple-element.40), kind=kOutput, calls=%fused_computation.5 | convolution fusion | flops 13428326400 | bytes 35389440 | tf_op jit(solution)/shard_map/bld,blf->df/dot_general | solution.py:287
  603.2 6.5 convolution_bitcast_fusion
  609.7 9.1 %fusion.18 = bf16[320,2560]{1,0:T(8,128)(2,1)} fusion(f32[320,2560]{1,0:T(8,128)S(1)} %convolution_bitcast_fusion, bf16[8,256,320]{2,1,0:T(8,128)(2,1)S(1)} %copy-done.3, bf16[8,256,2560]{2,1,0:T(8,128)(2,1)} %all-gather.9.cloned.1.call-done), kind=kOutput, calls=%fused_computation.32 | convolution fusion | flops 3357081600 | bytes 16711680 | tf_op jit(solution)/shard_map/blk,bld->kd/dot_general | solution.py:287
  618.8 19.6 %fusion.1 = bf16[2560,1280]{1,0:T(8,128)(2,1)} fusion(f32[2560,1280,1]{1,0,2:T(8,128)} %fusion.68, bf16[8,256,2560]{2,1,0:T(8,128)(2,1)S(1)} %bitcast.152, bf16[8,256,1280]{2,1,0:T(8,128)(2,1)} %get-tuple-element.39), kind=kOutput, calls=%fused_computation.3 | convolution fusion | flops 13428326400 | bytes 35389440 | tf_op jit(solution)/shard_map/bld,blf->df/dot_general | solution.py:287
  638.4 21.9 %fusion = bf16[1280,2560]{1,0:T(8,128)(2,1)} fusion(f32[1280,2560,1]{1,0,2:T(8,128)} %fusion.69, bf16[8,256,1280]{2,1,0:T(8,128)(2,1)} %get-tuple-element.41, bf16[8,256,2560]{2,1,0:T(8,128)(2,1)} %all-gather.11.cloned.1.call-done), kind=kOutput, calls=%fused_computation.1 | convolution fusion | flops 13428326400 | bytes 35389440 | tf_op jit(solution)/shard_map/blf,bld->fd/dot_general | solution.py:287
  660.4 4.0 fusion.46
  664.5 36.4 %all-reduce.6 = (f32[2560]{0:T(1024)}, bf16[160,2560]{1,0:T(8,128)(2,1)S(1)}) all-reduce(f32[2560]{0:T(1024)S(1)} %add.82, f32[160,2560]{1,0:T(8,128)} %slice.36), channel_id=1, replica_groups=mesh['tp'=8] {'tp'}, use_global_device_ids=true, to_apply=%region_14.0 | all-reduce | flops 412160 | bytes 2478080 | tf_op jit(solution)/shard_map/psum | solution.py:309
  700.9 0.9 slice_bitcast_fusion
  701.9 4.9 fusion.43
  706.8 1.7 pad_maximum_fusion
  708.5 1.7 pad_maximum_fusion.1
  (125 shorter events, 2.1 us)
Async XLA Ops:
  7.2 4.9 copy-start.9
  7.2 4.9 copy-start.14
  7.2 67.7 %all-gather.5.cloned.1.call-start = ((), (), s32[]{:S(2)}) async-start(), calls=%async_computation.4 | async-start | bytes 11796480 | tf_op jit(solution)/shard_map/all_gather | solution.py:266
  9.5 4.9 copy-start.16
  9.5 4.9 copy-start.18
  12.1 2.4 copy-start.20
  14.5 5.2 copy-start.11
  14.5 5.2 copy-start.12
  14.5 5.2 copy-start.13
  14.5 120.2 %all-gather.7.cloned.1.call-start = ((), (), s32[]{:S(2)}) async-start(), calls=%async_computation.5 | async-start | bytes 11796480 | tf_op jit(solution)/shard_map/all_gather | solution.py:266
  15.3 179.3 %all-gather.9.cloned.1.call-start = ((), (), s32[]{:S(2)}) async-start(), calls=%async_computation.6 | async-start | bytes 11796480 | tf_op jit(solution)/shard_map/all_gather | solution.py:267
  18.8 319.4 %all-gather.11.cloned.1.call-start = ((), (), s32[]{:S(2)}) async-start(), calls=%async_computation.7 | async-start | bytes 11796480 | tf_op jit(solution)/shard_map/all_gather | solution.py:267
  19.4 641.0 %reduce-scatter.17.cloned.1.call-start = ((), (), s32[]{:S(2)}) async-start(), calls=%async_computation.10 | async-start | bytes 6553600
  194.6 8.1 %copy-start.8 = (bf16[8,480,256]{2,1,0:T(8,128)(2,1)S(1)}, bf16[8,480,256]{2,1,0:T(8,128)(2,1)}, u32[]{:S(2)}) copy-start(bf16[8,480,256]{2,1,0:T(8,128)(2,1)} %copy-done.7) | copy-start | bytes 5898244
  194.6 21.7 %slice-start.9 = ((s8[10485760]{0:T(1024)(128)(4,1)}), s8[4194304]{0:T(1024)(128)(4,1)S(1)}, s32[]{:S(2)}) async-start(s8[10485760]{0:T(1024)(128)(4,1)} %bitcast.164), calls=%async_computation.21 | async-start | bytes 8388608
  194.6 21.7 %slice-start.15 = ((s8[6553600]{0:T(1024)(128)(4,1)}), s8[4194304]{0:T(1024)(128)(4,1)S(1)}, s32[]{:S(2)}) async-start(s8[6553600]{0:T(1024)(128)(4,1)} %bitcast.168), calls=%async_computation.27 | async-start | bytes 8388608
  202.7 13.6 %slice-start.10 = ((s8[10485760]{0:T(1024)(128)(4,1)}), s8[4194304]{0:T(1024)(128)(4,1)S(1)}, s32[]{:S(2)}) async-start(s8[10485760]{0:T(1024)(128)(4,1)} %bitcast.164), calls=%async_computation.22 | async-start | bytes 8388608
  202.7 13.6 %slice-start.11 = ((s8[10485760]{0:T(1024)(128)(4,1)}), s8[2097152]{0:T(1024)(128)(4,1)S(1)}, s32[]{:S(2)}) async-start(s8[10485760]{0:T(1024)(128)(4,1)} %bitcast.164), calls=%async_computation.23 | async-start | bytes 4194304
  202.8 13.6 %slice-start.16 = ((s8[6553600]{0:T(1024)(128)(4,1)}), s8[2359296]{0:T(1024)(128)(4,1)S(1)}, s32[]{:S(2)}) async-start(s8[6553600]{0:T(1024)(128)(4,1)} %bitcast.168), calls=%async_computation.28 | async-start | bytes 4718592
  202.8 30.0 %slice-start.17 = ((s8[6553600]{0:T(1024)(128)(4,1)}), s8[4194304]{0:T(1024)(128)(4,1)S(1)}, s32[]{:S(2)}) async-start(s8[6553600]{0:T(1024)(128)(4,1)} %bitcast.170), calls=%async_computation.29 | async-start | bytes 8388608
  216.4 16.4 %copy-start.6 = (bf16[8,256,480]{2,1,0:T(8,128)(2,1)}, bf16[8,256,480]{2,1,0:T(8,128)(2,1)S(1)}, u32[]{:S(2)}) copy-start(bf16[8,256,480]{2,1,0:T(8,128)(2,1)S(1)} %attn_bwd.2) | copy-start | bytes 5898244
  216.4 16.4 %slice-start.18 = ((s8[6553600]{0:T(1024)(128)(4,1)}), s8[2359296]{0:T(1024)(128)(4,1)S(1)}, s32[]{:S(2)}) async-start(s8[6553600]{0:T(1024)(128)(4,1)} %bitcast.170), calls=%async_computation.30 | async-start | bytes 4718592
  318.8 341.6 %reduce-scatter.19.cloned.1.call-start = ((), (), s32[]{:S(2)}) async-start(), calls=%async_computation.11 | async-start | bytes 6553600
  338.2 23.0 %slice-start.3 = ((s8[10485760]{0:T(1024)(128)(4,1)}), s8[4194304]{0:T(1024)(128)(4,1)S(1)}, s32[]{:S(2)}) async-start(s8[10485760]{0:T(1024)(128)(4,1)} %bitcast.149), calls=%async_computation.15 | async-start | bytes 8388608
  338.3 23.0 %slice-start.19 = ((s8[6553600]{0:T(1024)(128)(4,1)}), s8[4194304]{0:T(1024)(128)(4,1)S(1)}, s32[]{:S(2)}) async-start(s8[6553600]{0:T(1024)(128)(4,1)} %bitcast.172), calls=%async_computation.31 | async-start | bytes 8388608
  346.4 14.9 %slice-start.4 = ((s8[10485760]{0:T(1024)(128)(4,1)}), s8[4194304]{0:T(1024)(128)(4,1)S(1)}, s32[]{:S(2)}) async-start(s8[10485760]{0:T(1024)(128)(4,1)} %bitcast.149), calls=%async_computation.16 | async-start | bytes 8388608
  346.4 14.9 %slice-start.5 = ((s8[10485760]{0:T(1024)(128)(4,1)}), s8[2097152]{0:T(1024)(128)(4,1)S(1)}, s32[]{:S(2)}) async-start(s8[10485760]{0:T(1024)(128)(4,1)} %bitcast.149), calls=%async_computation.17 | async-start | bytes 4194304
  346.4 14.8 %slice-start.20 = ((s8[6553600]{0:T(1024)(128)(4,1)}), s8[2359296]{0:T(1024)(128)(4,1)S(1)}, s32[]{:S(2)}) async-start(s8[6553600]{0:T(1024)(128)(4,1)} %bitcast.172), calls=%async_computation.32 | async-start | bytes 4718592
  447.1 254.8 %reduce-scatter.15.cloned.1.call-start = ((), (), s32[]{:S(2)}) async-start(), calls=%async_computation.9 | async-start | bytes 6553600
  474.8 9.2 %copy-start.1 = (bf16[8,256,480]{2,1,0:T(8,128)(2,1)S(1)}, bf16[8,256,480]{2,1,0:T(8,128)(2,1)}, u32[]{:S(2)}) copy-start(bf16[8,256,480]{2,1,0:T(8,128)(2,1)} %copy-done) | copy-start | bytes 5898244
  474.9 227.0 %reduce-scatter.13.cloned.1.call-start = ((), (), s32[]{:S(2)}) async-start(), calls=%async_computation.8 | async-start | bytes 6553600
  522.5 19.9 %slice-start.12 = ((s8[10485760]{0:T(1024)(128)(4,1)}), s8[2097152]{0:T(1024)(128)(4,1)S(1)}, s32[]{:S(2)}) async-start(s8[10485760]{0:T(1024)(128)(4,1)} %bitcast.166), calls=%async_computation.24 | async-start | bytes 4194304
  522.6 19.9 %slice-start.13 = ((s8[10485760]{0:T(1024)(128)(4,1)}), s8[4194304]{0:T(1024)(128)(4,1)S(1)}, s32[]{:S(2)}) async-start(s8[10485760]{0:T(1024)(128)(4,1)} %bitcast.166), calls=%async_computation.25 | async-start | bytes 8388608
  522.6 19.8 %slice-start.14 = ((s8[10485760]{0:T(1024)(128)(4,1)}), s8[4194304]{0:T(1024)(128)(4,1)S(1)}, s32[]{:S(2)}) async-start(s8[10485760]{0:T(1024)(128)(4,1)} %bitcast.166), calls=%async_computation.26 | async-start | bytes 8388608
  522.6 40.0 %slice-start = ((s8[10485760]{0:T(1024)(128)(4,1)}), s8[4194304]{0:T(1024)(128)(4,1)S(1)}, s32[]{:S(2)}) async-start(s8[10485760]{0:T(1024)(128)(4,1)} %bitcast.147), calls=%async_computation.12 | async-start | bytes 8388608
  522.6 40.0 %slice-start.1 = ((s8[10485760]{0:T(1024)(128)(4,1)}), s8[4194304]{0:T(1024)(128)(4,1)S(1)}, s32[]{:S(2)}) async-start(s8[10485760]{0:T(1024)(128)(4,1)} %bitcast.147), calls=%async_computation.13 | async-start | bytes 8388608
  542.5 20.1 %slice-start.2 = ((s8[10485760]{0:T(1024)(128)(4,1)}), s8[2097152]{0:T(1024)(128)(4,1)S(1)}, s32[]{:S(2)}) async-start(s8[10485760]{0:T(1024)(128)(4,1)} %bitcast.147), calls=%async_computation.14 | async-start | bytes 4194304
  581.2 22.0 %copy-start.5 = (bf16[8,256,320]{2,1,0:T(8,128)(2,1)S(1)}, bf16[8,256,320]{2,1,0:T(8,128)(2,1)}, u32[]{:S(2)}) copy-start(bf16[8,256,320]{2,1,0:T(8,128)(2,1)} %copy-done.4) | copy-start | bytes 3932164
  603.2 6.5 copy-start.3
  603.2 15.6 %slice-start.6 = ((s8[10485760]{0:T(1024)(128)(4,1)}), s8[2097152]{0:T(1024)(128)(4,1)S(1)}, s32[]{:S(2)}) async-start(s8[10485760]{0:T(1024)(128)(4,1)} %bitcast.151), calls=%async_computation.18 | async-start | bytes 4194304
  603.2 15.6 %slice-start.7 = ((s8[10485760]{0:T(1024)(128)(4,1)}), s8[4194304]{0:T(1024)(128)(4,1)S(1)}, s32[]{:S(2)}) async-start(s8[10485760]{0:T(1024)(128)(4,1)} %bitcast.151), calls=%async_computation.19 | async-start | bytes 8388608
  609.7 9.1 %slice-start.8 = ((s8[10485760]{0:T(1024)(128)(4,1)}), s8[4194304]{0:T(1024)(128)(4,1)S(1)}, s32[]{:S(2)}) async-start(s8[10485760]{0:T(1024)(128)(4,1)} %bitcast.151), calls=%async_computation.20 | async-start | bytes 8388608
  638.4 21.9 %copy-start.10 = (bf16[16,32,2560]{2,1,0:T(8,128)(2,1)S(1)}, bf16[16,32,2560]{2,1,0:T(8,128)(2,1)}, u32[]{:S(2)}) copy-start(bf16[16,32,2560]{2,1,0:T(8,128)(2,1)} %param.10) | copy-start | bytes 7864324
  638.4 22.0 %copy-start.15 = (f32[2560]{0:T(1024)S(1)}, f32[2560]{0:T(1024)}, u32[]{:S(2)}) copy-start(f32[2560]{0:T(1024)} %param.12) | copy-start | bytes 30724
  638.4 22.0 %copy-start.17 = (f32[8,32]{1,0:T(8,128)S(1)}, f32[8,32]{1,0:T(8,128)}, u32[]{:S(2)}) copy-start(f32[8,32]{1,0:T(8,128)} %copy-done.16) | copy-start | bytes 3076
  638.4 22.0 %copy-start.19 = (f32[8,32]{1,0:T(8,128)S(1)}, f32[8,32]{1,0:T(8,128)}, u32[]{:S(2)}) copy-start(f32[8,32]{1,0:T(8,128)} %copy-done.18) | copy-start | bytes 3076
  638.4 22.0 %copy-start.21 = (f32[8,32]{1,0:T(8,128)S(1)}, f32[8,32]{1,0:T(8,128)}, u32[]{:S(2)}) copy-start(f32[8,32]{1,0:T(8,128)} %copy-done.20) | copy-start | bytes 3076
  638.4 22.0 %copy-start.23 = (f32[8,32]{1,0:T(8,128)S(1)}, f32[8,32]{1,0:T(8,128)}, u32[]{:S(2)}) copy-start(f32[8,32]{1,0:T(8,128)} %copy-done.22) | copy-start | bytes 3076
  (5 other events, 7.2 us)
Sparse Core Ops, SparseCore 0:
  14.6 60.2 all-gather.4
  77.3 57.4 all-gather.6
  137.2 57.3 all-gather.8
  196.3 57.3 all-gather.10
  318.9 55.5 reduce-scatter.16
  447.2 55.5 reduce-scatter.18
  505.7 55.5 reduce-scatter.14
  564.2 55.5 reduce-scatter.12
